TPU v7x, 128 devices: a whole 4x4x4 slice. The times are simulated.
128 devices in a mesh: step: 2 (over core), tile: 64 (over z, y, x).
Axes of the slice: x: 4, y: 4, z: 4, core: 2. Of those that a mesh axis runs over, the one named last changes fastest.
Arguments:
- latents: float32 [2, 8192, 3072], P('step', 'tile'), may hold values from -6 to 6
- start: float32 [8192, 3072], P('tile'), may hold values from -6 to 6
- cached_velocity: float32 [2, 8192, 3072], P('step', 'tile'), may hold values from -4 to 4
- shift: float32 [2, 3072], P('step'), may hold values from -3 to 3
- scale: float32 [2, 3072], P('step'), may hold values from -3 to 3
- gate: float32 [2, 3072], P('step'), may hold values from -10 to 10
- step_sizes: float32 [2], P('step'), may hold values from 0.1 to 0.5
- converged: int32 [2, 64], P(None, 'tile'), may hold values from 0 to 1, as said below
- neighbours: int32 [64, 4], P('tile'), may hold values from 0 to 1, as said below
- w_qkv: bfloat16 [3, 3072, 2048], P(None, None, 'step'), may hold values from -0.109375 to 0.109375
- q_gain: float32 [128], replicated, may hold values from 0.1 to 1.9
- k_gain: float32 [128], replicated, may hold values from 0.1 to 1.9
- w_out: bfloat16 [2048, 3072], P('step', 'tile'), may hold values from -0.5 to 0.5
Outputs:
- updated: float32 [2, 8192, 3072], P('step', 'tile')
- velocity: float32 [2, 8192, 3072], P('step', 'tile')
Inputs may be any that keep to these rules, and one draw needn't show every extreme that they name: For each tile the converged steps are the first ones of the window, at most 1 of them. `neighbours`: an entry is 0 wherever the grid of 16 rows of 4 tiles has no neighbour that way.
All inputs are finite; a program needn't handle non-finite values.
Results may differ from a plain program's by a relative error of at most 0.008.
Values may be sent and summed in bfloat16 or wider, within the bound.
No kernel may reach another device: no remote copies, remote signals or barrier semaphores. Data moves between devices by JAX's collectives and lax.ppermute only.
A program may use at most 128 MiB of HBM per device.

v0:
```python
import jax
import jax.numpy as jnp
from jax import lax
from jax.sharding import PartitionSpec as P

GRID_COLS = 4


def copy_for_each(value, axis):
    copies = jnp.broadcast_to(value, (lax.axis_size(axis), *value.shape))
    return lax.all_to_all(copies, axis, split_axis=0, concat_axis=0, tiled=True)


def laid_out(parts, dim):
    dims = list(parts.shape[1:])
    dims[dim] *= parts.shape[0]
    return jnp.moveaxis(parts, 0, dim).reshape(dims)


def gathered_copies(value, axis, dim):
    parts = copy_for_each(value, axis)
    return laid_out(parts, dim)


def shifted(value, axis, steps):
    count = lax.axis_size(axis)
    first, last = (max(0, -steps), min(count, count - steps))
    return lax.ppermute(value, axis, [(source, source + steps) for source in range(first, last)])


def in_blocks(value, dim, count):
    before, after = (value.shape[:dim], value.shape[dim + 1 :])
    return jnp.moveaxis(value.reshape(*before, count, -1, *after), dim, 0)


def sum_at_owner(value, axis, dim):
    parts = in_blocks(value, dim, lax.axis_size(axis))
    arrived = lax.all_to_all(parts, axis, split_axis=0, concat_axis=0, tiled=True)
    return arrived.astype(jnp.float32).sum(axis=0)


def entering(value, axis, join, neutral):
    place = lax.axis_index(axis)
    gathered = lax.all_gather(value.astype(jnp.bfloat16), axis)
    state = jnp.zeros_like(value) + jnp.asarray(neutral, value.dtype)

    def one(lap, state):
        return join(state, lax.dynamic_index_in_dim(gathered, lap, 0, False).astype(value.dtype))

    return lax.fori_loop(0, place, one, state)


def attend(queries, keys_all, values_all, key_mask, factor):
    scores = (
        jnp.einsum("sqhd,skhd->shqk", queries, keys_all, preferred_element_type=jnp.float32)
        * factor
    )
    expo = jnp.exp(scores) * key_mask
    probs = (expo / jnp.sum(expo, axis=-1, keepdims=True)).astype(jnp.bfloat16)
    attended = jnp.einsum("shqk,skhd->sqhd", probs, values_all, preferred_element_type=jnp.float32)
    return attended.astype(jnp.bfloat16)


def rms_gain(block, gain):
    return (
        block / jnp.sqrt(jnp.mean(block * block, axis=-1, keepdims=True) + 1e-06) * gain
    ).astype(jnp.bfloat16)


def add_terms(earlier, later):
    return earlier + later


def body(
    latents,
    start,
    cached_velocity,
    shift,
    scale,
    gate,
    step_sizes,
    converged,
    neighbours,
    w_qkv,
    q_gain,
    k_gain,
    w_out,
):
    tile_tokens = latents.shape[1]
    width = latents.shape[2]
    group_cols = w_qkv.shape[2]
    head_size = q_gain.shape[0]
    group_heads = group_cols // head_size
    step_count = converged.shape[0]
    own = latents[0]
    mean = jnp.mean(own, axis=-1, keepdims=True)
    var = jnp.mean(jnp.square(own - mean), axis=-1, keepdims=True)
    normed = ((own - mean) / jnp.sqrt(var + 1e-06) * (1.0 + scale) + shift).astype(jnp.bfloat16)[
        None
    ]
    block = gathered_copies(normed, "step", 0)
    count = block.shape[0]
    project_flat = block.reshape(count * tile_tokens, width)
    result = jnp.einsum("rd,cdf->crf", project_flat, w_qkv, preferred_element_type=jnp.float32)
    qkv = result.reshape(3, count, tile_tokens, group_cols)
    qkv = qkv.reshape(3, step_count, tile_tokens, group_heads, head_size)
    queries = rms_gain(qkv[0], q_gain)
    keys_own = rms_gain(qkv[1], k_gain)
    values_own = qkv[2].astype(jnp.bfloat16)
    stacked = jnp.stack([keys_own, values_own]).reshape(2, step_count, tile_tokens, group_cols)
    collected = [stacked]
    for offset in (1, -1, GRID_COLS, -GRID_COLS):
        collected.append(shifted(stacked, "tile", offset))
    joined = jnp.concatenate(collected, axis=2).reshape(
        2, step_count, 5 * tile_tokens, group_heads, head_size
    )
    key_mask = jnp.concatenate(
        [
            jnp.ones((tile_tokens,), jnp.float32),
            jnp.repeat(neighbours[0].astype(jnp.float32), tile_tokens),
        ]
    )
    factor = 1.0 / jnp.sqrt(jnp.float32(head_size))
    results = []
    for position in range(step_count):

        def fresh(_, position=position):
            return attend(
                queries[position : position + 1],
                joined[0, position : position + 1],
                joined[1, position : position + 1],
                key_mask,
                factor,
            )

        def blank(_, position=position):
            return jnp.zeros((1, tile_tokens, group_heads, head_size), jnp.bfloat16)

        results.append(lax.cond(converged[position, 0] > 0, blank, fresh, 0))
    attended = jnp.concatenate(results, axis=0)
    attended = attended.reshape(step_count, tile_tokens, group_cols)
    flat = attended.reshape(step_count * tile_tokens, group_cols)
    terms = jnp.dot(
        flat, lax.all_gather(w_out, "tile", axis=1, tiled=True), preferred_element_type=jnp.float32
    )
    terms = terms.reshape(step_count, tile_tokens, width)
    projected = sum_at_owner(terms.astype(jnp.bfloat16), "step", 0)
    here = lax.axis_index("step")
    flag = lax.dynamic_slice_in_dim(converged, here, 1, 0)[0, 0]
    velocity = jnp.where(flag > 0, cached_velocity, gate[:, None, :] * projected)
    scaled = step_sizes[:, None, None] * velocity
    prefix = entering(scaled, "step", add_terms, jnp.zeros_like(scaled))
    updated = start[None, :, :] + prefix
    return (updated, velocity)


def solution(mesh):
    placed = (
        P("step", "tile", None),
        P("tile", None),
        P("step", "tile", None),
        P("step", None),
        P("step", None),
        P("step", None),
        P("step"),
        P(None, "tile"),
        P("tile", None),
        P(None, None, "step"),
        P(),
        P(),
        P("step", "tile"),
    )
    return jax.shard_map(
        body,
        mesh=mesh,
        in_specs=placed,
        out_specs=(P("step", "tile", None), P("step", "tile", None)),
        check_vma=False,
    )
```

profile of v0, /device:TPU:1, one launch (start us, length us, event | category | flops | bytes accessed | tf_op | source)
XLA Modules:
  0.0 156.8 jit_solution(7559792582649957298)
XLA Ops:
  8.0 1.6 %reduce_sum.65 = f32[128]{0:T(128)S(1)} reduce(f32[1,128,3072]{2,1,0:T(8,128)} %param.19, f32[]{:T(128)} %constant.42.clone.1), dimensions={0,2}, to_apply=%region_0.0 | reduce | flops 393088 | bytes 1573380 | tf_op jit(solution)/shard_map/reduce_sum | solution.py:96
  10.5 6.0 %all_to_all.10 = bf16[2,1,128,3072]{3,2,1,0:T(8,128)(2,1)S(1)} all-to-all(bf16[2,1,128,3072]{3,2,1,0:T(8,128)(2,1)S(1)} %broadcast_in_dim.10), channel_id=1, replica_groups=mesh['step'=2,'tile'=64] {'step'}, dimensions={0} | all-to-all | bytes 3145728 | tf_op jit(solution)/shard_map/all_to_all | solution.py:11
  16.5 9.0 %convolution_bitcast_fusion = f32[3,256,1024]{2,1,0:T(8,128)S(1)} fusion(bf16[256,3072,1]{1,0,2:T(8,128)(2,1)S(1)} %bitcast.134, bf16[3,3072,1024]{2,1,0:T(8,128)(2,1)} %param.28), kind=kOutput, calls=%fused_computation.30 | convolution fusion | flops 4831838208 | bytes 23592960 | tf_op jit(solution)/shard_map/rd,cdf->crf/dot_general | solution.py:104
  29.2 1.3 pad_maximum_fusion
  30.5 4.2 %collective-permute-start = (bf16[2,2,128,1024]{2,3,1,0:T(8,128)(2,1)S(1)}, bf16[2,2,128,1024]{2,3,1,0:T(8,128)(2,1)}, u32[]{:S(2)}, u32[]{:S(2)}) collective-permute-start(bf16[2,2,128,1024]{2,3,1,0:T(8,128)(2,1)S(1)} %get-tuple-element.101), channel_id=1, source_target_pairs={{0,1},{1,2},{2,3},{3,4},{4,5},{5,6},{6,7},{7,8},{8,9},{9,10},{10,1... | collective-permute-start | bytes 3145736 | tf_op jit(solution)/shard_map/ppermute | solution.py:28
  36.0 6.3 %collective-permute-start.2 = (bf16[2,2,128,1024]{2,3,1,0:T(8,128)(2,1)S(1)}, bf16[2,2,128,1024]{2,3,1,0:T(8,128)(2,1)}, u32[]{:S(2)}, u32[]{:S(2)}) collective-permute-start(bf16[2,2,128,1024]{2,3,1,0:T(8,128)(2,1)S(1)} %get-tuple-element.101), channel_id=1, source_target_pairs={{0,4},{1,5},{2,6},{3,7},{4,8},{5,9},{6,10},{7,11},{8,12},{9,13},{1... | collective-permute-start | bytes 3145736 | tf_op jit(solution)/shard_map/ppermute | solution.py:28
  47.9 10.3 %collective-permute-done = bf16[2,2,128,1024]{2,3,1,0:T(8,128)(2,1)} collective-permute-done((bf16[2,2,128,1024]{2,3,1,0:T(8,128)(2,1)S(1)}, bf16[2,2,128,1024]{2,3,1,0:T(8,128)(2,1)}, u32[]{:S(2)}, u32[]{:S(2)}) %collective-permute-start) | collective-permute-done | bytes 1048608 | tf_op jit(solution)/shard_map/ppermute | solution.py:28
  58.1 2.4 %constant_dynamic-update-slice_fusion.3 = bf16[2,2,640,1024]{2,3,1,0:T(8,128)(2,1)} fusion(bf16[2,2,640,1024]{2,3,1,0:T(8,128)(2,1)} %get-tuple-element.102, bf16[2,2,128,1024]{2,3,1,0:T(8,128)(2,1)} %collective-permute-done), kind=kLoop, calls=%fused_computation.56 | loop fusion | bytes 2097152
  60.5 3.8 %collective-permute-done.1 = bf16[2,2,128,1024]{2,3,1,0:T(8,128)(2,1)} collective-permute-done((bf16[2,2,128,1024]{2,3,1,0:T(8,128)(2,1)S(1)}, bf16[2,2,128,1024]{2,3,1,0:T(8,128)(2,1)}, u32[]{:S(2)}, u32[]{:S(2)}) %collective-permute-start.1) | collective-permute-done | bytes 1048608 | tf_op jit(solution)/shard_map/ppermute | solution.py:28
  64.3 2.4 %constant_dynamic-update-slice_fusion.2 = bf16[2,2,640,1024]{2,3,1,0:T(8,128)(2,1)} fusion(bf16[2,2,640,1024]{2,3,1,0:T(8,128)(2,1)} %constant_dynamic-update-slice_fusion.3, bf16[2,2,128,1024]{2,3,1,0:T(8,128)(2,1)} %collective-permute-done.1), kind=kLoop, calls=%fused_computation.55 | loop fusion | bytes 2097152
  66.7 19.0 %collective-permute-done.2 = bf16[2,2,128,1024]{2,3,1,0:T(8,128)(2,1)} collective-permute-done((bf16[2,2,128,1024]{2,3,1,0:T(8,128)(2,1)S(1)}, bf16[2,2,128,1024]{2,3,1,0:T(8,128)(2,1)}, u32[]{:S(2)}, u32[]{:S(2)}) %collective-permute-start.2) | collective-permute-done | bytes 1048608 | tf_op jit(solution)/shard_map/ppermute | solution.py:28
  85.6 2.3 %constant_dynamic-update-slice_fusion.1 = bf16[2,2,640,1024]{2,3,1,0:T(8,128)(2,1)} fusion(bf16[2,2,640,1024]{2,3,1,0:T(8,128)(2,1)} %constant_dynamic-update-slice_fusion.2, bf16[2,2,128,1024]{2,3,1,0:T(8,128)(2,1)} %collective-permute-done.2), kind=kLoop, calls=%fused_computation.54 | loop fusion | bytes 2097152
  88.0 2.3 %constant_dynamic-update-slice_fusion = bf16[2,2,640,1024]{2,3,1,0:T(8,128)(2,1)} fusion(bf16[2,2,640,1024]{2,3,1,0:T(8,128)(2,1)} %constant_dynamic-update-slice_fusion.1, bf16[2,2,128,1024]{2,3,1,0:T(8,128)(2,1)} %collective-permute-done.3), kind=kLoop, calls=%fused_computation.53 | loop fusion | bytes 2097152 | tf_op jit(solution)/shard_map/concatenate | solution.py:114
  90.3 12.1 %conditional.3 = (bf16[1,128,8,128]{3,1,2,0:T(8,128)(2,1)S(1)}) conditional(s32[]{:T(128)} %bitcast.31, (bf16[2,128,8,128]{3,1,2,0:T(8,128)(2,1)S(1)}, bf16[2,2,640,8,128]{2,4,3,1,0:T(8,128)(2,1)}, f32[640]{0:T(1024)S(1)}) %tuple.67, () %tuple.26), branch_computations={%region_7.0_spmd, %region_9.0_spmd} | conditional | flops 340261888 | bytes 18889224 | solution.py:139
  90.3 7.9 %copy.42 = bf16[2,2,640,8,128]{4,2,3,1,0:T(8,128)(2,1)} copy(bf16[2,2,640,8,128]{2,4,3,1,0:T(8,128)(2,1)} %get-tuple-element.78) | data formatting | bytes 10485760 | tf_op jit(solution)/shard_map
  98.2 2.1 %fusion.8 = (f32[8,128]{1,0:T(8,128)S(1)}, f32[8,128,640]{2,1,0:T(8,128)S(1)}) fusion(f32[640]{0:T(1024)S(1)} %get-tuple-element.39, bf16[2,2,640,8,128]{4,2,3,1,0:T(8,128)(2,1)} %copy.42, bf16[2,128,8,128]{3,1,2,0:T(8,128)(2,1)S(1)} %get-tuple-element.37), kind=kOutput, calls=%fused_computation.14 | convolution fusion | flops 169737216 | bytes 4202496 | tf_op jit(solution)/shard_map/cond/branch_0_fun/sqhd,skhd->shqk/dot_general | solution.py:55
  100.3 2.1 %fusion.12 = bf16[1,128,8,128]{3,1,2,0:T(8,128)(2,1)S(1)} fusion(bf16[2,2,640,8,128]{4,2,3,1,0:T(8,128)(2,1)} %copy.42, f32[8,128,640]{2,1,0:T(8,128)S(1)} %get-tuple-element.97, f32[8,128]{1,0:T(8,128)S(1)} %get-tuple-element.96, f32[640]{0:T(1024)S(1)} %get-tuple-element.39), kind=kOutput, calls=%fused_computation.20 | convolution fusion | flops 170524672 | bytes 4200960 | tf_op jit(solution)/shard_map/cond/branch_0_fun/shqk,skhd->sqhd/dot_general | solution.py:60
  102.4 19.8 %all-gather.4.cloned.1.call-done = bf16[1024,3072]{0,1:T(8,128)(2,1)} async-done(((bf16[1024,48]{0,1:T(8,128)(2,1)}), bf16[1024,3072]{0,1:T(8,128)(2,1)}) %all-gather.4.cloned.1.call-update) | async-done | bytes 6291472 | tf_op jit(solution)/shard_map/all_gather | solution.py:144
  122.2 4.7 %fusion.21 = bf16[2,1,128,3072]{3,2,1,0:T(8,128)(2,1)S(1)} fusion(bf16[1024,3072]{0,1:T(8,128)(2,1)} %all-gather.4.cloned.1.call-done, bf16[1,128,8,128]{3,1,2,0:T(8,128)(2,1)S(1)} %get-tuple-element.154, bf16[1,128,8,128]{3,1,2,0:T(8,128)(2,1)S(1)} %get-tuple-element.153), kind=kOutput, calls=%fused_computation.28 | convolution fusion | flops 1611661312 | bytes 8388608 | tf_op jit(solution)/shard_map/dot_general | solution.py:143
  126.9 5.9 %all_to_all.11 = bf16[2,1,128,3072]{3,2,1,0:T(8,128)(2,1)S(1)} all-to-all(bf16[2,1,128,3072]{3,2,1,0:T(8,128)(2,1)S(1)} %fusion.21), channel_id=1, replica_groups=mesh['step'=2,'tile'=64] {'step'}, dimensions={0} | all-to-all | bytes 3145728 | tf_op jit(solution)/shard_map/all_to_all | solution.py:38
  133.1 1.7 %multiply_convert_fusion = (bf16[1,128,3072]{2,1,0:T(8,128)(2,1)}, f32[1,128,3072]{2,1,0:T(8,128)}) fusion(f32[]{:T(128)} %bitcast.128, f32[1,128,3072]{2,1,0:T(8,128)S(1)} %copy-done.4, f32[128,3072]{1,0:T(8,128)S(1)} %convert_reduce_fusion, f32[3072]{0:T(1024)S(1)} %bitcast.140, pred[]{:T(512)} %bitcast.15), kind=kLoop, calls=%fused_computation.35 | loop fusion | flops 1572864 | bytes 5517317 | tf_op jit(solution)/shard_map/convert_element_type | solution.py:44
  134.8 12.1 %all-gather.6.cloned.1.call-done = bf16[2,128,3072]{2,1,0:T(8,128)(2,1)} async-done(((bf16[1,128,3072]{2,1,0:T(8,128)(2,1)}), bf16[2,128,3072]{2,1,0:T(8,128)(2,1)}) %all-gather.6.cloned.1.call-update) | async-done | bytes 1572880 | tf_op jit(solution)/shard_map/all_gather | solution.py:44
  147.0 1.6 %while.10 = (s32[]{:T(128)}, f32[1,128,3072]{2,1,0:T(8,128)S(1)}, s32[]{:T(128)}, bf16[2,1,128,3072]{3,2,1,0:T(8,128)(2,1)}, s32[]{:T(128)}, /*index=5*/s32[]{:T(128)}, s32[]{:T(128)}) while((s32[]{:T(128)}, f32[1,128,3072]{2,1,0:T(8,128)S(1)}, s32[]{:T(128)}, bf16[2,1,128,3072]{3,2,1,0:T(8,128)(2,1)}, s32[]{:T(128)}, ...), condition=%wide.region_12.13_spmd, body=%wide.region_11.12_spmd.sunk | while | flops 786437 | bytes 3932275 | solution.py:50
  147.0 1.6 %convert_add_fusion.2 = f32[1,128,3072]{2,1,0:T(8,128)S(1)} fusion(f32[1,128,3072]{2,1,0:T(8,128)S(1)} %get-tuple-element.140, bf16[2,1,128,3072]{3,2,1,0:T(8,128)(2,1)} %get-tuple-element.149, s32[]{:T(128)S(6)} %select_n.23), kind=kLoop, calls=%fused_computation.24.clone.1 | loop fusion | flops 786432 | bytes 3932164 | tf_op jit(solution)/shard_map/while/body/add | solution.py:71
  (59 shorter events, 11.4 us)
Async XLA Ops:
  7.2 21.7 %copy-start = (f32[128]{0:T(128)S(1)}, f32[128]{0:T(128)}, u32[]{:S(2)}) copy-start(f32[128]{0:T(128)} %param.30) | copy-start | bytes 1540
  7.2 2.4 %copy-start.2 = (f32[1,128,3072]{2,1,0:T(8,128)S(1)}, f32[1,128,3072]{2,1,0:T(8,128)}, u32[]{:S(2)}) copy-start(f32[1,128,3072]{2,1,0:T(8,128)} %param.19) | copy-start | bytes 4718596
  7.2 2.7 %copy-start.6 = (f32[1,3072]{1,0:T(1,128)S(1)}, f32[1,3072]{1,0:T(1,128)}, u32[]{:S(2)}) copy-start(f32[1,3072]{1,0:T(1,128)} %param.23) | copy-start | bytes 36868
  7.2 2.7 %copy-start.5 = (f32[1,3072]{1,0:T(1,128)S(1)}, f32[1,3072]{1,0:T(1,128)}, u32[]{:S(2)}) copy-start(f32[1,3072]{1,0:T(1,128)} %param.22) | copy-start | bytes 36868
  7.2 114.9 %all-gather.4.cloned.1.call-start = ((), (), s32[]{:S(2)}) async-start(), calls=%async_computation.2 | async-start | bytes 6389760 | tf_op jit(solution)/shard_map/all_gather | solution.py:144
  7.9 138.9 %all-gather.6.cloned.1.call-start = ((), (), s32[]{:S(2)}) async-start(), calls=%async_computation.3 | async-start | bytes 2359296 | tf_op jit(solution)/shard_map/all_gather | solution.py:44
  28.9 14.7 %copy-start.10 = (s32[1,4]{1,0:T(1,128)S(1)}, s32[1,4]{1,0:T(1,128)}, u32[]{:S(2)}) copy-start(s32[1,4]{1,0:T(1,128)} %param.27) | copy-start | bytes 52
  29.2 15.1 %copy-start.8 = (s32[2,1]{0,1:T(1,128)S(1)}, s32[2,1]{0,1:T(1,128)}, u32[]{:S(2)}) copy-start(s32[2,1]{0,1:T(1,128)} %param.26) | copy-start | bytes 28
  29.2 18.3 %copy-start.9 = (f32[128]{0:T(128)S(1)}, f32[128]{0:T(128)}, u32[]{:S(2)}) copy-start(f32[128]{0:T(128)} %param.29) | copy-start | bytes 1540
  30.5 27.6 %collective-permute-start = (bf16[2,2,128,1024]{2,3,1,0:T(8,128)(2,1)S(1)}, bf16[2,2,128,1024]{2,3,1,0:T(8,128)(2,1)}, u32[]{:S(2)}, u32[]{:S(2)}) collective-permute-start(bf16[2,2,128,1024]{2,3,1,0:T(8,128)(2,1)S(1)} %get-tuple-element.101), channel_id=1, source_target_pairs={{0,1},{1,2},{2,3},{3,4},{4,5},{5,6},{6,7},{7,8},{8,9},{9,10},{10,1... | collective-permute-start | bytes 3145736 | tf_op jit(solution)/shard_map/ppermute | solution.py:28
  34.7 29.6 %collective-permute-start.1 = (bf16[2,2,128,1024]{2,3,1,0:T(8,128)(2,1)S(1)}, bf16[2,2,128,1024]{2,3,1,0:T(8,128)(2,1)}, u32[]{:S(2)}, u32[]{:S(2)}) collective-permute-start(bf16[2,2,128,1024]{2,3,1,0:T(8,128)(2,1)S(1)} %get-tuple-element.101), channel_id=1, source_target_pairs={{1,0},{2,1},{3,2},{4,3},{5,4},{6,5},{7,6},{8,7},{9,8},{10,9},{11,1... | collective-permute-start | bytes 3145736 | tf_op jit(solution)/shard_map/ppermute | solution.py:28
  36.0 49.6 %collective-permute-start.2 = (bf16[2,2,128,1024]{2,3,1,0:T(8,128)(2,1)S(1)}, bf16[2,2,128,1024]{2,3,1,0:T(8,128)(2,1)}, u32[]{:S(2)}, u32[]{:S(2)}) collective-permute-start(bf16[2,2,128,1024]{2,3,1,0:T(8,128)(2,1)S(1)} %get-tuple-element.101), channel_id=1, source_target_pairs={{0,4},{1,5},{2,6},{3,7},{4,8},{5,9},{6,10},{7,11},{8,12},{9,13},{1... | collective-permute-start | bytes 3145736 | tf_op jit(solution)/shard_map/ppermute | solution.py:28
  42.3 45.7 %collective-permute-start.3 = (bf16[2,2,128,1024]{2,3,1,0:T(8,128)(2,1)S(1)}, bf16[2,2,128,1024]{2,3,1,0:T(8,128)(2,1)}, u32[]{:S(2)}, u32[]{:S(2)}) collective-permute-start(bf16[2,2,128,1024]{2,3,1,0:T(8,128)(2,1)S(1)} %get-tuple-element.101), channel_id=1, source_target_pairs={{4,0},{5,1},{6,2},{7,3},{8,4},{9,5},{10,6},{11,7},{12,8},{13,9},{1... | collective-permute-start | bytes 3145736 | tf_op jit(solution)/shard_map/ppermute | solution.py:28
  126.9 6.2 %copy-start.4 = (f32[1,128,3072]{2,1,0:T(8,128)S(1)}, f32[1,128,3072]{2,1,0:T(8,128)}, u32[]{:S(2)}) copy-start(f32[1,128,3072]{2,1,0:T(8,128)} %param.21) | copy-start | bytes 4718596
  126.9 6.2 %copy-start.7 = (f32[1,3072]{1,0:T(1,128)S(1)}, f32[1,3072]{1,0:T(1,128)}, u32[]{:S(2)}) copy-start(f32[1,3072]{1,0:T(1,128)} %param.24) | copy-start | bytes 36868
  147.0 1.7 %copy-start.3 = (f32[128,3072]{1,0:T(8,128)S(1)}, f32[128,3072]{1,0:T(8,128)}, u32[]{:S(2)}) copy-start(f32[128,3072]{1,0:T(8,128)} %param.20) | copy-start | bytes 4718596
  148.7 1.3 copy-start.1
Sparse Core Ops, SparseCore 0:
  10.8 111.3 all-gather.3
  134.9 11.9 all-gather.5
where the time goes:
time: 158 us; the launch traced here: 157 us
  waiting for transfers between devices  65.6 us (42%)
  local copies, waits for them, and re-layouts  21.4 us (14%)
  matrix products  17.9 us (11%)
  between operations  17 us (11%)
  starting transfers between devices  13.1 us (8%)
  blocking collectives  11.9 us (8%)
  other arithmetic  10 us (6%)
    ppermute x4, waiting for transfers between devices, shifted(): lax.ppermute(value, axis, [(source, source + steps) for source in range(f...  33 us
    all_gather x1, waiting for transfers between devices, body(): lax.all_gather(w_out, 'tile', axis=1, tiled=True)  19.8 us
    ppermute x4, starting transfers between devices, shifted(): lax.ppermute(value, axis, [(source, source + steps) for source in range(f...  13 us
    all_gather x1, waiting for transfers between devices, entering(): gathered = lax.all_gather(value.astype(jnp.bfloat16), axis)  12.1 us
    dot_general x1, matrix products, body(): jnp.einsum('rd,cdf->crf', project_flat, w_qkv, preferred_element_type=jnp...  8.97 us
    another operation x2, local copies, waits for them, and re-layouts  7.92 us
    unnamed x27, local copies, waits for them, and re-layouts  7.54 us
    all_to_all x1, blocking collectives, copy_for_each(): return lax.all_to_all(copies, axis, split_axis=0, concat_axis=0, tiled=True)  6.01 us
  transfers between devices with their start and end apart: 6, of which 5 were waited for; matrix products, arithmetic and copies ran while one was open for 25% of the time, Pallas kernels for 0%

commit v1 on v0

--- a/solution.py
+++ b/solution.py
@@ -141,7 +141,11 @@
     attended = attended.reshape(step_count, tile_tokens, group_cols)
     flat = attended.reshape(step_count * tile_tokens, group_cols)
     terms = jnp.dot(
-        flat, lax.all_gather(w_out, "tile", axis=1, tiled=True), preferred_element_type=jnp.float32
+        flat,
+        jnp.concatenate(
+            lax.all_to_all(jnp.stack([w_out] * lax.axis_size("tile")), "tile", 0, 0), axis=1
+        ),
+        preferred_element_type=jnp.float32,
     )
     terms = terms.reshape(step_count, tile_tokens, width)
     projected = sum_at_owner(terms.astype(jnp.bfloat16), "step", 0)

time: 158 us -> 220 us (1.39)
  waiting for transfers between devices: 65.6 us -> 113 us
  starting transfers between devices: 13.1 us -> 24 us
  local copies, waits for them, and re-layouts: 21.4 us -> 24.9 us
    ppermute x4, waiting for transfers between devices: 33 us -> 82.8 us  [shifted(): lax.ppermute(value, axis, [(source, source + steps) for source in range(f...]
    all_gather x1 -> x0, waiting for transfers between devices: 19.8 us -> none  [body(): lax.all_gather(w_out, 'tile', axis=1, tiled=True)]
    all_gather x1, waiting for transfers between devices: 12.1 us -> 30 us  [entering(): gathered = lax.all_gather(value.astype(jnp.bfloat16), axis)]
    all_to_all x0 -> x1, starting transfers between devices: none -> 11.5 us  [body(): lax.all_to_all(jnp.stack([w_out] * lax.axis_size('tile')), 'tile', 0, 0)]
    another operation x2 -> x3, local copies, waits for them, and re-layouts: 7.92 us -> 11.3 us
    unnamed x27 -> x29, local copies, waits for them, and re-layouts: 7.54 us -> 7.57 us
  transfers between devices with their start and end apart: 6 -> 6, of which waited for: 5 -> 3; matrix products, arithmetic and copies ran while one was open for 25% -> 17% of each run, Pallas kernels for 0% -> 0%
where the time goes in v1:
time: 220 us; the launch traced here: 219 us
  waiting for transfers between devices  113 us (51%)
  local copies, waits for them, and re-layouts  24.9 us (11%)
  starting transfers between devices  24 us (11%)
  matrix products  17.9 us (8%)
  between operations  17 us (8%)
  blocking collectives  12 us (5%)
  other arithmetic  10.1 us (5%)
    ppermute x4, waiting for transfers between devices, shifted(): lax.ppermute(value, axis, [(source, source + steps) for source in range(f...  82.8 us
    all_gather x1, waiting for transfers between devices, entering(): gathered = lax.all_gather(value.astype(jnp.bfloat16), axis)  30 us
    ppermute x4, starting transfers between devices, shifted(): lax.ppermute(value, axis, [(source, source + steps) for source in range(f...  12.5 us
    all_to_all x1, starting transfers between devices, body(): lax.all_to_all(jnp.stack([w_out] * lax.axis_size('tile')), 'tile', 0, 0)  11.5 us
    dot_general x1, matrix products, body(): jnp.einsum('rd,cdf->crf', project_flat, w_qkv, preferred_element_type=jnp...  9.02 us
    another operation x2, local copies, waits for them, and re-layouts  7.88 us
    unnamed x29, local copies, waits for them, and re-layouts  7.57 us
    all_to_all x1, blocking collectives, copy_for_each(): return lax.all_to_all(copies, axis, split_axis=0, concat_axis=0, tiled=True)  6.01 us
  transfers between devices with their start and end apart: 6, of which 3 were waited for; matrix products, arithmetic and copies ran while one was open for 17% of the time, Pallas kernels for 0%

profile of v1, /device:TPU:1, one launch (start us, length us, event | category | flops | bytes accessed | tf_op | source)
XLA Modules:
  0.0 219.0 jit_solution(17727364482030104567)
XLA Ops:
  7.2 1.7 reduce_sum.65
  10.0 6.0 %all_to_all.15 = bf16[2,1,128,3072]{3,2,1,0:T(8,128)(2,1)S(1)} all-to-all(bf16[2,1,128,3072]{3,2,1,0:T(8,128)(2,1)S(1)} %broadcast_in_dim.10), channel_id=1, replica_groups=mesh['step'=2,'tile'=64] {'step'}, dimensions={0} | all-to-all | bytes 3145728 | tf_op jit(solution)/shard_map/all_to_all | solution.py:11
  16.0 3.5 %stack.5 = bf16[64,1024,48]{1,2,0:T(8,128)(2,1)} broadcast(bf16[1024,48]{0,1:T(8,128)(2,1)S(1)} %copy-done.5), dimensions={1,2} | broadcast | bytes 6389760 | tf_op jit(solution)/shard_map/stack | solution.py:146
  19.5 11.5 %all-to-all-start.1 = ((bf16[64,1024,48]{1,2,0:T(8,128)(2,1)}), bf16[64,1024,48]{1,2,0:T(8,128)(2,1)}, u32[]{:S(2)}, u32[]{:S(2)}) async-start(bf16[64,1024,48]{1,2,0:T(8,128)(2,1)} %stack.5), calls=%async_computation.1 | async-start | bytes 12582912 | tf_op jit(solution)/shard_map/all_to_all | solution.py:146
  31.0 9.0 %convolution_bitcast_fusion = f32[3,256,1024]{2,1,0:T(8,128)S(1)} fusion(bf16[256,3072,1]{1,0,2:T(8,128)(2,1)S(1)} %bitcast.133, bf16[3,3072,1024]{2,1,0:T(8,128)(2,1)} %param.28), kind=kOutput, calls=%fused_computation.28 | convolution fusion | flops 4831838208 | bytes 23592960 | tf_op jit(solution)/shard_map/rd,cdf->crf/dot_general | solution.py:104
  43.8 1.3 pad_maximum_fusion
  45.1 3.8 %collective-permute-start = (bf16[2,2,128,1024]{2,3,1,0:T(8,128)(2,1)S(1)}, bf16[2,2,128,1024]{2,3,1,0:T(8,128)(2,1)}, u32[]{:S(2)}, u32[]{:S(2)}) collective-permute-start(bf16[2,2,128,1024]{2,3,1,0:T(8,128)(2,1)S(1)} %get-tuple-element.101), channel_id=1, source_target_pairs={{0,1},{1,2},{2,3},{3,4},{4,5},{5,6},{6,7},{7,8},{8,9},{9,10},{10,1... | collective-permute-start | bytes 3145736 | tf_op jit(solution)/shard_map/ppermute | solution.py:28
  50.2 6.1 %collective-permute-start.2 = (bf16[2,2,128,1024]{2,3,1,0:T(8,128)(2,1)S(1)}, bf16[2,2,128,1024]{2,3,1,0:T(8,128)(2,1)}, u32[]{:S(2)}, u32[]{:S(2)}) collective-permute-start(bf16[2,2,128,1024]{2,3,1,0:T(8,128)(2,1)S(1)} %get-tuple-element.101), channel_id=1, source_target_pairs={{0,4},{1,5},{2,6},{3,7},{4,8},{5,9},{6,10},{7,11},{8,12},{9,13},{1... | collective-permute-start | bytes 3145736 | tf_op jit(solution)/shard_map/ppermute | solution.py:28
  61.9 75.1 %collective-permute-done = bf16[2,2,128,1024]{2,3,1,0:T(8,128)(2,1)} collective-permute-done((bf16[2,2,128,1024]{2,3,1,0:T(8,128)(2,1)S(1)}, bf16[2,2,128,1024]{2,3,1,0:T(8,128)(2,1)}, u32[]{:S(2)}, u32[]{:S(2)}) %collective-permute-start) | collective-permute-done | bytes 1048608 | tf_op jit(solution)/shard_map/ppermute | solution.py:28
  137.0 2.3 %constant_dynamic-update-slice_fusion.3 = bf16[2,2,640,1024]{2,3,1,0:T(8,128)(2,1)} fusion(bf16[2,2,640,1024]{2,3,1,0:T(8,128)(2,1)} %get-tuple-element.102, bf16[2,2,128,1024]{2,3,1,0:T(8,128)(2,1)} %collective-permute-done), kind=kLoop, calls=%fused_computation.54 | loop fusion | bytes 2097152
  139.3 2.3 %constant_dynamic-update-slice_fusion.2 = bf16[2,2,640,1024]{2,3,1,0:T(8,128)(2,1)} fusion(bf16[2,2,640,1024]{2,3,1,0:T(8,128)(2,1)} %constant_dynamic-update-slice_fusion.3, bf16[2,2,128,1024]{2,3,1,0:T(8,128)(2,1)} %collective-permute-done.1), kind=kLoop, calls=%fused_computation.53 | loop fusion | bytes 2097152
  141.6 7.7 %collective-permute-done.2 = bf16[2,2,128,1024]{2,3,1,0:T(8,128)(2,1)} collective-permute-done((bf16[2,2,128,1024]{2,3,1,0:T(8,128)(2,1)S(1)}, bf16[2,2,128,1024]{2,3,1,0:T(8,128)(2,1)}, u32[]{:S(2)}, u32[]{:S(2)}) %collective-permute-start.2) | collective-permute-done | bytes 1048608 | tf_op jit(solution)/shard_map/ppermute | solution.py:28
  149.3 2.3 %constant_dynamic-update-slice_fusion.1 = bf16[2,2,640,1024]{2,3,1,0:T(8,128)(2,1)} fusion(bf16[2,2,640,1024]{2,3,1,0:T(8,128)(2,1)} %constant_dynamic-update-slice_fusion.2, bf16[2,2,128,1024]{2,3,1,0:T(8,128)(2,1)} %collective-permute-done.2), kind=kLoop, calls=%fused_computation.52 | loop fusion | bytes 2097152
  151.6 2.3 %constant_dynamic-update-slice_fusion = bf16[2,2,640,1024]{2,3,1,0:T(8,128)(2,1)} fusion(bf16[2,2,640,1024]{2,3,1,0:T(8,128)(2,1)} %constant_dynamic-update-slice_fusion.1, bf16[2,2,128,1024]{2,3,1,0:T(8,128)(2,1)} %collective-permute-done.3), kind=kLoop, calls=%fused_computation.51 | loop fusion | bytes 2097152 | tf_op jit(solution)/shard_map/concatenate | solution.py:114
  154.0 12.2 %conditional.3 = (bf16[1,128,8,128]{3,1,2,0:T(8,128)(2,1)S(1)}) conditional(s32[]{:T(128)} %bitcast.31, (bf16[2,128,8,128]{3,1,2,0:T(8,128)(2,1)S(1)}, bf16[2,2,640,8,128]{2,4,3,1,0:T(8,128)(2,1)}, f32[640]{0:T(1024)S(1)}) %tuple.65, () %tuple.26), branch_computations={%region_7.0_spmd, %region_9.0_spmd} | conditional | flops 340261888 | bytes 18889224 | solution.py:139
  154.0 7.8 %copy.45 = bf16[2,2,640,8,128]{4,2,3,1,0:T(8,128)(2,1)} copy(bf16[2,2,640,8,128]{2,4,3,1,0:T(8,128)(2,1)} %get-tuple-element.78) | data formatting | bytes 10485760 | tf_op jit(solution)/shard_map
  161.8 2.1 fusion.8
  163.9 2.1 fusion.12
  166.2 4.7 %fusion.16 = bf16[2,1,128,3072]{3,2,1,0:T(8,128)(2,1)S(1)} fusion(bf16[1024,3072,1]{0,1,2:T(8,128)(2,1)} %bitcast.34, bf16[1,128,8,128]{3,1,2,0:T(8,128)(2,1)S(1)} %get-tuple-element.154, bf16[1,128,8,128]{3,1,2,0:T(8,128)(2,1)S(1)} %get-tuple-element.153), kind=kOutput, calls=%fused_computation.26 | convolution fusion | flops 1611661312 | bytes 8388608 | tf_op jit(solution)/shard_map/dot_general | solution.py:143
  170.9 6.0 %all_to_all.16 = bf16[2,1,128,3072]{3,2,1,0:T(8,128)(2,1)S(1)} all-to-all(bf16[2,1,128,3072]{3,2,1,0:T(8,128)(2,1)S(1)} %fusion.16), channel_id=1, replica_groups=mesh['step'=2,'tile'=64] {'step'}, dimensions={0} | all-to-all | bytes 3145728 | tf_op jit(solution)/shard_map/all_to_all | solution.py:38
  177.2 1.7 multiply_convert_fusion
  178.9 30.0 %all-gather.3.cloned.1.call-done = bf16[2,128,3072]{2,1,0:T(8,128)(2,1)} async-done(((bf16[1,128,3072]{2,1,0:T(8,128)(2,1)}), bf16[2,128,3072]{2,1,0:T(8,128)(2,1)}) %all-gather.3.cloned.1.call-update) | async-done | bytes 1572880 | tf_op jit(solution)/shard_map/all_gather | solution.py:44
  209.1 1.6 while.10
  209.2 1.6 convert_add_fusion.2
  (61 shorter events, 10.8 us)
Async XLA Ops:
  7.2 36.3 %copy-start = (f32[128]{0:T(128)S(1)}, f32[128]{0:T(128)}, u32[]{:S(2)}) copy-start(f32[128]{0:T(128)} %param.30) | copy-start | bytes 1540
  7.2 1.9 copy-start.2
  7.2 2.2 %copy-start.7 = (f32[1,3072]{1,0:T(1,128)S(1)}, f32[1,3072]{1,0:T(1,128)}, u32[]{:S(2)}) copy-start(f32[1,3072]{1,0:T(1,128)} %param.23) | copy-start | bytes 36868
  7.2 2.2 %copy-start.6 = (f32[1,3072]{1,0:T(1,128)S(1)}, f32[1,3072]{1,0:T(1,128)}, u32[]{:S(2)}) copy-start(f32[1,3072]{1,0:T(1,128)} %param.22) | copy-start | bytes 36868
  9.8 6.2 %copy-start.5 = (bf16[1024,48]{0,1:T(8,128)(2,1)S(1)}, bf16[1024,48]{0,1:T(8,128)(2,1)}, u32[]{:S(2)}) copy-start(bf16[1024,48]{0,1:T(8,128)(2,1)} %param.31) | copy-start | bytes 294916
  19.5 146.7 %all-to-all-start.1 = ((bf16[64,1024,48]{1,2,0:T(8,128)(2,1)}), bf16[64,1024,48]{1,2,0:T(8,128)(2,1)}, u32[]{:S(2)}, u32[]{:S(2)}) async-start(bf16[64,1024,48]{1,2,0:T(8,128)(2,1)} %stack.5), calls=%async_computation.1 | async-start | bytes 12582912 | tf_op jit(solution)/shard_map/all_to_all | solution.py:146
  30.9 178.0 %all-gather.3.cloned.1.call-start = ((), (), s32[]{:S(2)}) async-start(), calls=%async_computation.3 | async-start | bytes 2359296 | tf_op jit(solution)/shard_map/all_gather | solution.py:44
  43.4 14.2 %copy-start.11 = (s32[1,4]{1,0:T(1,128)S(1)}, s32[1,4]{1,0:T(1,128)}, u32[]{:S(2)}) copy-start(s32[1,4]{1,0:T(1,128)} %param.27) | copy-start | bytes 52
  43.7 14.5 %copy-start.9 = (s32[2,1]{0,1:T(1,128)S(1)}, s32[2,1]{0,1:T(1,128)}, u32[]{:S(2)}) copy-start(s32[2,1]{0,1:T(1,128)} %param.26) | copy-start | bytes 28
  43.7 17.8 %copy-start.10 = (f32[128]{0:T(128)S(1)}, f32[128]{0:T(128)}, u32[]{:S(2)}) copy-start(f32[128]{0:T(128)} %param.29) | copy-start | bytes 1540
  45.1 91.9 %collective-permute-start = (bf16[2,2,128,1024]{2,3,1,0:T(8,128)(2,1)S(1)}, bf16[2,2,128,1024]{2,3,1,0:T(8,128)(2,1)}, u32[]{:S(2)}, u32[]{:S(2)}) collective-permute-start(bf16[2,2,128,1024]{2,3,1,0:T(8,128)(2,1)S(1)} %get-tuple-element.101), channel_id=1, source_target_pairs={{0,1},{1,2},{2,3},{3,4},{4,5},{5,6},{6,7},{7,8},{8,9},{9,10},{10,1... | collective-permute-start | bytes 3145736 | tf_op jit(solution)/shard_map/ppermute | solution.py:28
  48.9 90.4 %collective-permute-start.1 = (bf16[2,2,128,1024]{2,3,1,0:T(8,128)(2,1)S(1)}, bf16[2,2,128,1024]{2,3,1,0:T(8,128)(2,1)}, u32[]{:S(2)}, u32[]{:S(2)}) collective-permute-start(bf16[2,2,128,1024]{2,3,1,0:T(8,128)(2,1)S(1)} %get-tuple-element.101), channel_id=1, source_target_pairs={{1,0},{2,1},{3,2},{4,3},{5,4},{6,5},{7,6},{8,7},{9,8},{10,9},{11,1... | collective-permute-start | bytes 3145736 | tf_op jit(solution)/shard_map/ppermute | solution.py:28
  50.2 99.1 %collective-permute-start.2 = (bf16[2,2,128,1024]{2,3,1,0:T(8,128)(2,1)S(1)}, bf16[2,2,128,1024]{2,3,1,0:T(8,128)(2,1)}, u32[]{:S(2)}, u32[]{:S(2)}) collective-permute-start(bf16[2,2,128,1024]{2,3,1,0:T(8,128)(2,1)S(1)} %get-tuple-element.101), channel_id=1, source_target_pairs={{0,4},{1,5},{2,6},{3,7},{4,8},{5,9},{6,10},{7,11},{8,12},{9,13},{1... | collective-permute-start | bytes 3145736 | tf_op jit(solution)/shard_map/ppermute | solution.py:28
  56.3 95.3 %collective-permute-start.3 = (bf16[2,2,128,1024]{2,3,1,0:T(8,128)(2,1)S(1)}, bf16[2,2,128,1024]{2,3,1,0:T(8,128)(2,1)}, u32[]{:S(2)}, u32[]{:S(2)}) collective-permute-start(bf16[2,2,128,1024]{2,3,1,0:T(8,128)(2,1)S(1)} %get-tuple-element.101), channel_id=1, source_target_pairs={{4,0},{5,1},{6,2},{7,3},{8,4},{9,5},{10,6},{11,7},{12,8},{13,9},{1... | collective-permute-start | bytes 3145736 | tf_op jit(solution)/shard_map/ppermute | solution.py:28
  170.9 6.3 %copy-start.4 = (f32[1,128,3072]{2,1,0:T(8,128)S(1)}, f32[1,128,3072]{2,1,0:T(8,128)}, u32[]{:S(2)}) copy-start(f32[1,128,3072]{2,1,0:T(8,128)} %param.21) | copy-start | bytes 4718596
  170.9 6.3 %copy-start.8 = (f32[1,3072]{1,0:T(1,128)S(1)}, f32[1,3072]{1,0:T(1,128)}, u32[]{:S(2)}) copy-start(f32[1,3072]{1,0:T(1,128)} %param.24) | copy-start | bytes 36868
  209.1 1.7 copy-start.3
  210.8 1.3 copy-start.1
Sparse Core Ops, SparseCore 0:
  179.1 29.8 all-gather.2
